TPU v7x, 128 devices: a whole 4x4x4 slice. The times are simulated.
128 devices in a mesh: box: 16 (over y, z), panel: 8 (over x, core).
Axes of the slice: x: 4, y: 4, z: 4, core: 2. Of those that a mesh axis runs over, the one named last changes fastest.
Arguments:
- field_start: float32 [4096, 4096], P('box', 'panel'), may hold values from -6 to 6
- fluid_mask: int32 [4096, 4096], P('box', 'panel'), may hold values 0 or 1
- base_visc: float32 [4096, 4096], P('box', 'panel'), may hold values from 0.02 to 0.1
- panel_cell: int32 [16384], P(('box', 'panel')), may hold values from 0 to 131071
- amplitude: bfloat16 [16384, 4096], P('box', 'panel'), may hold values from 0.049804688 to 0.5
- delay_bin: int32 [16384, 4096], P('box', 'panel'), may hold values from 0 to 2044
Outputs:
- field_end: float32 [4096, 4096], P('box', 'panel')
- signals: float32 [4096, 2048], P('panel', 'box')
Inputs may be any that keep to these rules, and one draw needn't show every extreme that they name: `panel_cell`: an index, row-major, into the 256 x 512 block of the device that owns the panel.
All inputs are finite; a program needn't handle non-finite values. No bound on the sum of `fluid_mask` on one device may be relied on, other than what follows from the above.
Results may differ from a plain program's by a relative error of at most 0.0029.
Values may be sent and summed in bfloat16 or wider, within the bound.
A program may use at most 64 MiB of HBM per device.

v0:
```python
import math
import jax
import jax.numpy as jnp
from jax import lax
from jax.sharding import PartitionSpec as P

STEPS = 4
NB = 2048


def padded(x, sides, width):
    edges = {}
    for axis, dim in sides:
        peers, length = (lax.axis_size(axis), x.shape[dim])
        up = [(i, (i + 1) % peers) for i in range(peers - 1)]
        last = lax.slice_in_dim(x, length - width, length, axis=dim)
        initial = lax.slice_in_dim(x, 0, width, axis=dim)
        edges[dim] = (
            lax.ppermute(last, axis, up),
            lax.ppermute(initial, axis, [(b, a) for a, b in up]),
        )
    done = []
    for _, dim in sides:
        low, high = edges[dim]
        around = [(width, width) if d in done else (0, 0) for d in range(x.ndim)]
        x = jnp.concatenate([jnp.pad(low, around), x, jnp.pad(high, around)], axis=dim)
        done.append(dim)
    return x


def advance(ext, mask_c, base_c):
    center = ext[1:-1, 1:-1]
    west = ext[:-2, 1:-1]
    east = ext[2:, 1:-1]
    south = ext[1:-1, :-2]
    north = ext[1:-1, 2:]
    grad_x = 0.5 * (east - west)
    grad_y = 0.5 * (north - south)
    grad_norm = jnp.sqrt(grad_x * grad_x + grad_y * grad_y)
    viscosity = base_c + 0.05 * grad_norm / (1.0 + grad_norm)
    update = center + viscosity * (east + west + north + south - 4.0 * center)
    update = update - 0.15 * (center - west) - 0.1 * (center - south)
    return mask_c * update


def signal_terms(amplitude, delay_bin, sample):
    panels, observers = amplitude.shape
    groups = NB // 128
    width = math.gcd(observers, max(1, 32768 // panels))
    blocks = observers // width
    amp_blocks = amplitude.reshape(panels, blocks, width).transpose(1, 0, 2)
    bin_blocks = delay_bin.reshape(panels, blocks, width).transpose(1, 0, 2)
    high_ids = jnp.arange(groups, dtype=jnp.int32)
    low_ids = jnp.arange(128, dtype=jnp.int32)

    def one_block(pair):
        amp_rows, bin_rows = pair
        weight = (amp_rows.astype(jnp.float32)[None, :, :] * sample[:, :, None]).astype(
            jnp.bfloat16
        )
        high = bin_rows // 128
        low = bin_rows % 128
        chosen = high[:, :, None] == high_ids[None, None, :]
        left = jnp.where(chosen[None], weight[:, :, :, None], jnp.zeros((), jnp.bfloat16))
        right = (low[:, :, None] == low_ids[None, None, :]).astype(jnp.bfloat16)
        binned = jnp.einsum("tpoh,pol->othl", left, right, preferred_element_type=jnp.float32)
        binned = binned.reshape(width, STEPS, NB)
        total = binned[:, 0, :]
        for step in range(1, STEPS):
            total = total + jnp.pad(binned[:, step, : NB - step], ((0, 0), (step, 0)))
        return total

    result = lax.map(one_block, (amp_blocks, bin_blocks))
    return result.reshape(observers, NB)


def on_device(field_start, fluid_mask, base_visc, panel_cell, amplitude, delay_bin):
    maskf = fluid_mask.astype(jnp.float32)
    taken = []
    field = field_start
    for step in range(STEPS):
        extended = padded(field, (("box", 0), ("panel", 1)), 1)
        field = advance(extended, maskf, base_visc)
        taken.append(field.reshape(-1)[panel_cell])
    sample = jnp.stack(taken)
    every = lax.all_gather(sample, ("box", "panel"), axis=1, tiled=True)
    amp_all = lax.all_to_all(amplitude, "box", split_axis=1, concat_axis=0, tiled=True)
    bin_all = lax.all_to_all(delay_bin, "box", split_axis=1, concat_axis=0, tiled=True)
    finished = signal_terms(amp_all, bin_all, every)
    signals = lax.all_to_all(finished, "box", split_axis=1, concat_axis=0, tiled=True)
    return (field, signals)


def solution(mesh):
    placed = (
        P("box", "panel"),
        P("box", "panel"),
        P("box", "panel"),
        P(("box", "panel")),
        P("box", "panel"),
        P("box", "panel"),
    )
    return jax.shard_map(
        on_device,
        mesh=mesh,
        in_specs=placed,
        out_specs=(P("box", "panel"), P("panel", "box")),
        check_vma=False,
    )
```

profile of v0, /device:TPU:0, one launch (start us, length us, event | category | flops | bytes accessed | tf_op | source)
XLA Modules:
  0.0 311.0 jit_solution(857162247917352217)
XLA Ops:
  2.8 4.6 %collective-permute-start.1 = (f32[1,512]{1,0:T(1,128)S(1)}, f32[1,512]{1,0:T(1,128)S(1)}, u32[]{:S(2)}, u32[]{:S(2)}) collective-permute-start(f32[1,512]{1,0:T(1,128)S(1)} %get-tuple-element.136), channel_id=1, source_target_pairs={{0,8},{8,16},{16,24},{24,32},{32,40},{40,48},{48,56},{56,64},{64,7... | collective-permute-start | bytes 6152 | tf_op jit(solution)/shard_map/ppermute | solution.py:19
  8.4 1.3 collective-permute-start.2
  9.7 3.0 collective-permute-start.3
  12.8 2.3 copy.28
  15.1 10.3 %all-to-all-start.1 = ((bf16[1024,16,32]{0,2,1:T(8,128)(2,1)}), bf16[1024,16,32]{0,2,1:T(8,128)(2,1)S(1)}, u32[]{:S(2)}, u32[]{:S(2)}) async-start(bf16[1024,16,32]{0,2,1:T(8,128)(2,1)} %bitcast.105), calls=%async_computation.1 | async-start | bytes 2097152 | tf_op jit(solution)/shard_map/all_to_all | solution.py:87
  26.2 1.3 collective-permute-start.4
  27.5 4.5 %collective-permute-start.5 = (f32[1,512]{1,0:T(1,128)S(1)}, f32[1,512]{1,0:T(1,128)S(1)}, u32[]{:S(2)}, u32[]{:S(2)}) collective-permute-start(f32[1,512]{1,0:T(1,128)S(1)} %get-tuple-element.132), channel_id=1, source_target_pairs={{0,8},{8,16},{16,24},{24,32},{32,40},{40,48},{48,56},{56,64},{64,7... | collective-permute-start | bytes 6152 | tf_op jit(solution)/shard_map/ppermute | solution.py:19
  32.2 1.3 collective-permute-start.6
  33.5 3.0 collective-permute-start.7
  36.5 2.9 copy.26
  43.0 4.0 %collective-permute-start.11 = (f32[256,1]{1,0:T(8,128)S(1)}, f32[256,1]{1,0:T(8,128)S(1)}, u32[]{:S(2)}, u32[]{:S(2)}) collective-permute-start(f32[256,1]{1,0:T(8,128)S(1)} %get-tuple-element.125), channel_id=1, source_target_pairs={{0,1},{1,2},{2,3},{3,4},{4,5},{5,6},{6,7},{8,9},{9,10},{10,11},{11... | collective-permute-start | bytes 3080 | tf_op jit(solution)/shard_map/ppermute | solution.py:19
  48.0 8.8 %all-to-all-start = ((s32[1024,16,32]{0,2,1:T(8,128)}), s32[1024,16,32]{0,2,1:T(8,128)S(1)}, u32[]{:S(2)}, u32[]{:S(2)}) async-start(s32[1024,16,32]{0,2,1:T(8,128)} %bitcast), calls=%async_computation | async-start | bytes 4194304 | tf_op jit(solution)/shard_map/all_to_all | solution.py:88
  58.8 4.5 %collective-permute-start.9 = (f32[1,512]{1,0:T(1,128)S(1)}, f32[1,512]{1,0:T(1,128)S(1)}, u32[]{:S(2)}, u32[]{:S(2)}) collective-permute-start(f32[1,512]{1,0:T(1,128)S(1)} %get-tuple-element.128), channel_id=1, source_target_pairs={{0,8},{8,16},{16,24},{24,32},{32,40},{40,48},{48,56},{56,64},{64,7... | collective-permute-start | bytes 6152 | tf_op jit(solution)/shard_map/ppermute | solution.py:19
  63.4 5.8 %collective-permute-done.8 = f32[1,512]{1,0:T(1,128)S(1)} collective-permute-done((f32[1,512]{1,0:T(1,128)S(1)}, f32[1,512]{1,0:T(1,128)S(1)}, u32[]{:S(2)}, u32[]{:S(2)}) %collective-permute-start.8) | collective-permute-done | bytes 2080 | tf_op jit(solution)/shard_map/ppermute | solution.py:20
  69.2 2.7 fusion.44
  72.8 1.3 collective-permute-start.14
  74.1 11.1 %collective-permute-start.15 = (f32[256,1]{1,0:T(8,128)}, f32[256,1]{1,0:T(8,128)}, u32[]{:S(2)}, u32[]{:S(2)}) collective-permute-start(f32[256,1]{1,0:T(8,128)} %get-tuple-element.121), channel_id=1, source_target_pairs={{0,1},{1,2},{2,3},{3,4},{4,5},{5,6},{6,7},{8,9},{9,10},{10,11},{11... | collective-permute-start | bytes 3080 | tf_op jit(solution)/shard_map/ppermute | solution.py:19
  87.0 4.5 %collective-permute-start.13 = (f32[1,512]{1,0:T(1,128)S(1)}, f32[1,512]{1,0:T(1,128)S(1)}, u32[]{:S(2)}, u32[]{:S(2)}) collective-permute-start(f32[1,512]{1,0:T(1,128)S(1)} %get-tuple-element.124), channel_id=1, source_target_pairs={{0,8},{8,16},{16,24},{24,32},{32,40},{40,48},{48,56},{56,64},{64,7... | collective-permute-start | bytes 6152 | tf_op jit(solution)/shard_map/ppermute | solution.py:19
  91.6 2.0 copy.36
  93.6 2.5 gather_fusion
  96.2 2.0 copy.37
  98.1 2.5 gather_fusion.1
  100.6 2.0 copy.38
  102.6 2.6 gather_fusion.2
  105.3 2.8 fusion.26
  110.9 48.7 %all_gather.3 = f32[4,16384]{1,0:T(4,128)S(1)} all-gather(f32[4,128]{1,0:T(4,128)S(1)} %pad_maximum_fusion.24), channel_id=1, replica_groups=mesh['box'=16,'panel'=8] {'box','panel'}, dimensions={1}, use_global_device_ids=true | all-gather | bytes 264192 | tf_op jit(solution)/shard_map/all_gather | solution.py:86
  159.6 2.8 copy.29
  162.4 2.6 reshape.98
  165.0 2.6 copy.27
  167.6 3.0 reshape.97
  170.6 125.7 %while.13 = (s32[]{:T(128)}, f32[16,2,2048]{2,1,0:T(2,128)S(1)}, s32[16,16384,2]{1,2,0:T(2,128)S(1)}, bf16[16,16384,2]{1,2,0:T(2,128)(2,1)}, f32[4,16384]{1,0:T(4,128)S(1)}, /*index=5*/s32[]{:T(128)}) while((s32[]{:T(128)}, f32[16,2,2048]{2,1,0:T(2,128)S(1)}, s32[16,16384,2]{1,2,0:T(2,128)S(1)}, bf16[16,16384,2]{1,2,0:T(2,128)(2,1)}, ...), condition=%wide.region_1.2_spmd.clone, body=%wide.region_0.1_spmd.clone.sunk | while | flops 544616448 | bytes 11714449 | solution.py:73
  173.2 4.9 %fusion.114 = f32[2,4,16,128]{3,2,1,0:T(8,128)S(1)} fusion(s32[16384,2]{0,1:T(2,128)S(1)} %get-tuple-element.170, bf16[4,16384,2,16]{1,3,0,2:T(8,128)(2,1)S(1)} %fusion.113), kind=kOutput, calls=%fused_computation.8.clone.3 | convolution fusion | flops 541065216 | bytes 4390912 | tf_op jit(solution)/shard_map/while/body/eval_jaxpr/tpoh,pol->othl/dot_general | solution.py:66
  181.1 4.9 %fusion.114 = f32[2,4,16,128]{3,2,1,0:T(8,128)S(1)} fusion(s32[16384,2]{0,1:T(2,128)S(1)} %get-tuple-element.170, bf16[4,16384,2,16]{1,3,0,2:T(8,128)(2,1)S(1)} %fusion.113), kind=kOutput, calls=%fused_computation.8.clone.3 | convolution fusion | flops 541065216 | bytes 4390912 | tf_op jit(solution)/shard_map/while/body/eval_jaxpr/tpoh,pol->othl/dot_general | solution.py:66
  188.9 4.9 %fusion.114 = f32[2,4,16,128]{3,2,1,0:T(8,128)S(1)} fusion(s32[16384,2]{0,1:T(2,128)S(1)} %get-tuple-element.170, bf16[4,16384,2,16]{1,3,0,2:T(8,128)(2,1)S(1)} %fusion.113), kind=kOutput, calls=%fused_computation.8.clone.3 | convolution fusion | flops 541065216 | bytes 4390912 | tf_op jit(solution)/shard_map/while/body/eval_jaxpr/tpoh,pol->othl/dot_general | solution.py:66
  196.8 4.9 %fusion.114 = f32[2,4,16,128]{3,2,1,0:T(8,128)S(1)} fusion(s32[16384,2]{0,1:T(2,128)S(1)} %get-tuple-element.170, bf16[4,16384,2,16]{1,3,0,2:T(8,128)(2,1)S(1)} %fusion.113), kind=kOutput, calls=%fused_computation.8.clone.3 | convolution fusion | flops 541065216 | bytes 4390912 | tf_op jit(solution)/shard_map/while/body/eval_jaxpr/tpoh,pol->othl/dot_general | solution.py:66
  204.7 4.9 %fusion.114 = f32[2,4,16,128]{3,2,1,0:T(8,128)S(1)} fusion(s32[16384,2]{0,1:T(2,128)S(1)} %get-tuple-element.170, bf16[4,16384,2,16]{1,3,0,2:T(8,128)(2,1)S(1)} %fusion.113), kind=kOutput, calls=%fused_computation.8.clone.3 | convolution fusion | flops 541065216 | bytes 4390912 | tf_op jit(solution)/shard_map/while/body/eval_jaxpr/tpoh,pol->othl/dot_general | solution.py:66
  212.5 4.9 %fusion.114 = f32[2,4,16,128]{3,2,1,0:T(8,128)S(1)} fusion(s32[16384,2]{0,1:T(2,128)S(1)} %get-tuple-element.170, bf16[4,16384,2,16]{1,3,0,2:T(8,128)(2,1)S(1)} %fusion.113), kind=kOutput, calls=%fused_computation.8.clone.3 | convolution fusion | flops 541065216 | bytes 4390912 | tf_op jit(solution)/shard_map/while/body/eval_jaxpr/tpoh,pol->othl/dot_general | solution.py:66
  220.4 4.9 %fusion.114 = f32[2,4,16,128]{3,2,1,0:T(8,128)S(1)} fusion(s32[16384,2]{0,1:T(2,128)S(1)} %get-tuple-element.170, bf16[4,16384,2,16]{1,3,0,2:T(8,128)(2,1)S(1)} %fusion.113), kind=kOutput, calls=%fused_computation.8.clone.3 | convolution fusion | flops 541065216 | bytes 4390912 | tf_op jit(solution)/shard_map/while/body/eval_jaxpr/tpoh,pol->othl/dot_general | solution.py:66
  228.2 4.9 %fusion.114 = f32[2,4,16,128]{3,2,1,0:T(8,128)S(1)} fusion(s32[16384,2]{0,1:T(2,128)S(1)} %get-tuple-element.170, bf16[4,16384,2,16]{1,3,0,2:T(8,128)(2,1)S(1)} %fusion.113), kind=kOutput, calls=%fused_computation.8.clone.3 | convolution fusion | flops 541065216 | bytes 4390912 | tf_op jit(solution)/shard_map/while/body/eval_jaxpr/tpoh,pol->othl/dot_general | solution.py:66
  236.1 4.9 %fusion.114 = f32[2,4,16,128]{3,2,1,0:T(8,128)S(1)} fusion(s32[16384,2]{0,1:T(2,128)S(1)} %get-tuple-element.170, bf16[4,16384,2,16]{1,3,0,2:T(8,128)(2,1)S(1)} %fusion.113), kind=kOutput, calls=%fused_computation.8.clone.3 | convolution fusion | flops 541065216 | bytes 4390912 | tf_op jit(solution)/shard_map/while/body/eval_jaxpr/tpoh,pol->othl/dot_general | solution.py:66
  243.9 4.9 %fusion.114 = f32[2,4,16,128]{3,2,1,0:T(8,128)S(1)} fusion(s32[16384,2]{0,1:T(2,128)S(1)} %get-tuple-element.170, bf16[4,16384,2,16]{1,3,0,2:T(8,128)(2,1)S(1)} %fusion.113), kind=kOutput, calls=%fused_computation.8.clone.3 | convolution fusion | flops 541065216 | bytes 4390912 | tf_op jit(solution)/shard_map/while/body/eval_jaxpr/tpoh,pol->othl/dot_general | solution.py:66
  251.8 4.9 %fusion.114 = f32[2,4,16,128]{3,2,1,0:T(8,128)S(1)} fusion(s32[16384,2]{0,1:T(2,128)S(1)} %get-tuple-element.170, bf16[4,16384,2,16]{1,3,0,2:T(8,128)(2,1)S(1)} %fusion.113), kind=kOutput, calls=%fused_computation.8.clone.3 | convolution fusion | flops 541065216 | bytes 4390912 | tf_op jit(solution)/shard_map/while/body/eval_jaxpr/tpoh,pol->othl/dot_general | solution.py:66
  259.7 4.9 %fusion.114 = f32[2,4,16,128]{3,2,1,0:T(8,128)S(1)} fusion(s32[16384,2]{0,1:T(2,128)S(1)} %get-tuple-element.170, bf16[4,16384,2,16]{1,3,0,2:T(8,128)(2,1)S(1)} %fusion.113), kind=kOutput, calls=%fused_computation.8.clone.3 | convolution fusion | flops 541065216 | bytes 4390912 | tf_op jit(solution)/shard_map/while/body/eval_jaxpr/tpoh,pol->othl/dot_general | solution.py:66
  267.5 4.9 %fusion.114 = f32[2,4,16,128]{3,2,1,0:T(8,128)S(1)} fusion(s32[16384,2]{0,1:T(2,128)S(1)} %get-tuple-element.170, bf16[4,16384,2,16]{1,3,0,2:T(8,128)(2,1)S(1)} %fusion.113), kind=kOutput, calls=%fused_computation.8.clone.3 | convolution fusion | flops 541065216 | bytes 4390912 | tf_op jit(solution)/shard_map/while/body/eval_jaxpr/tpoh,pol->othl/dot_general | solution.py:66
  275.4 4.9 %fusion.114 = f32[2,4,16,128]{3,2,1,0:T(8,128)S(1)} fusion(s32[16384,2]{0,1:T(2,128)S(1)} %get-tuple-element.170, bf16[4,16384,2,16]{1,3,0,2:T(8,128)(2,1)S(1)} %fusion.113), kind=kOutput, calls=%fused_computation.8.clone.3 | convolution fusion | flops 541065216 | bytes 4390912 | tf_op jit(solution)/shard_map/while/body/eval_jaxpr/tpoh,pol->othl/dot_general | solution.py:66
  283.2 4.9 %fusion.114 = f32[2,4,16,128]{3,2,1,0:T(8,128)S(1)} fusion(s32[16384,2]{0,1:T(2,128)S(1)} %get-tuple-element.170, bf16[4,16384,2,16]{1,3,0,2:T(8,128)(2,1)S(1)} %fusion.113), kind=kOutput, calls=%fused_computation.8.clone.3 | convolution fusion | flops 541065216 | bytes 4390912 | tf_op jit(solution)/shard_map/while/body/eval_jaxpr/tpoh,pol->othl/dot_general | solution.py:66
  291.1 4.9 %fusion.114 = f32[2,4,16,128]{3,2,1,0:T(8,128)S(1)} fusion(s32[16384,2]{0,1:T(2,128)S(1)} %get-tuple-element.170, bf16[4,16384,2,16]{1,3,0,2:T(8,128)(2,1)S(1)} %fusion.113), kind=kOutput, calls=%fused_computation.8.clone.3 | convolution fusion | flops 541065216 | bytes 4390912 | tf_op jit(solution)/shard_map/while/body/eval_jaxpr/tpoh,pol->othl/dot_general | solution.py:66
  296.6 13.7 %all_to_all.51 = f32[32,16,128]{2,0,1:T(8,128)S(1)} all-to-all(f32[32,16,128]{2,0,1:T(8,128)S(1)} %copy.30), channel_id=1, replica_groups=mesh['box'=16,'panel'=8] {'box'}, dimensions={1} | all-to-all | bytes 524288 | tf_op jit(solution)/shard_map/all_to_all | solution.py:90
  (282 shorter events, 62.8 us)
Async XLA Ops:
  0.6 24.7 %copy-start.7 = (f32[256,512]{1,0:T(8,128)S(1)}, f32[256,512]{1,0:T(8,128)}, u32[]{:S(2)}) copy-start(f32[256,512]{1,0:T(8,128)} %param.8) | copy-start | bytes 1572868
  0.6 24.7 %copy-start = (f32[256,512]{1,0:T(8,128)S(1)}, f32[256,512]{1,0:T(8,128)}, u32[]{:S(2)}) copy-start(f32[256,512]{1,0:T(8,128)} %param.10) | copy-start | bytes 1572868
  0.7 24.7 %copy-start.1 = (s32[256,512]{1,0:T(8,128)S(1)}, s32[256,512]{1,0:T(8,128)}, u32[]{:S(2)}) copy-start(s32[256,512]{1,0:T(8,128)} %param.9) | copy-start | bytes 1572868
  1.5 23.8 %collective-permute-start = (f32[1,512]{1,0:T(1,128)S(1)}, f32[1,512]{1,0:T(1,128)S(1)}, u32[]{:S(2)}, u32[]{:S(2)}) collective-permute-start(f32[1,512]{1,0:T(1,128)S(1)} %get-tuple-element.135), channel_id=1, source_target_pairs={{8,0},{16,8},{24,16},{32,24},{40,32},{48,40},{56,48},{64,56},{72,6... | collective-permute-start | bytes 6152 | tf_op jit(solution)/shard_map/ppermute | solution.py:20
  2.8 22.6 %collective-permute-start.1 = (f32[1,512]{1,0:T(1,128)S(1)}, f32[1,512]{1,0:T(1,128)S(1)}, u32[]{:S(2)}, u32[]{:S(2)}) collective-permute-start(f32[1,512]{1,0:T(1,128)S(1)} %get-tuple-element.136), channel_id=1, source_target_pairs={{0,8},{8,16},{16,24},{24,32},{32,40},{40,48},{48,56},{56,64},{64,7... | collective-permute-start | bytes 6152 | tf_op jit(solution)/shard_map/ppermute | solution.py:19
  8.4 16.9 %collective-permute-start.2 = (f32[256,1]{1,0:T(8,128)S(1)}, f32[256,1]{1,0:T(8,128)S(1)}, u32[]{:S(2)}, u32[]{:S(2)}) collective-permute-start(f32[256,1]{1,0:T(8,128)S(1)} %get-tuple-element.134), channel_id=1, source_target_pairs={{1,0},{2,1},{3,2},{4,3},{5,4},{6,5},{7,6},{9,8},{10,9},{11,10},{12... | collective-permute-start | bytes 3080 | tf_op jit(solution)/shard_map/ppermute | solution.py:20
  9.7 15.6 %collective-permute-start.3 = (f32[256,1]{1,0:T(8,128)S(1)}, f32[256,1]{1,0:T(8,128)S(1)}, u32[]{:S(2)}, u32[]{:S(2)}) collective-permute-start(f32[256,1]{1,0:T(8,128)S(1)} %get-tuple-element.133), channel_id=1, source_target_pairs={{0,1},{1,2},{2,3},{3,4},{4,5},{5,6},{6,7},{8,9},{9,10},{10,11},{11... | collective-permute-start | bytes 3080 | tf_op jit(solution)/shard_map/ppermute | solution.py:19
  15.1 32.0 %all-to-all-start.1 = ((bf16[1024,16,32]{0,2,1:T(8,128)(2,1)}), bf16[1024,16,32]{0,2,1:T(8,128)(2,1)S(1)}, u32[]{:S(2)}, u32[]{:S(2)}) async-start(bf16[1024,16,32]{0,2,1:T(8,128)(2,1)} %bitcast.105), calls=%async_computation.1 | async-start | bytes 2097152 | tf_op jit(solution)/shard_map/all_to_all | solution.py:87
  26.2 20.9 %copy-start.2 = (f32[256,512]{1,0:T(8,128)}, f32[256,512]{1,0:T(8,128)S(1)}, u32[]{:S(2)}) copy-start(f32[256,512]{1,0:T(8,128)S(1)} %fusion.80) | copy-start | bytes 1572868
  26.2 13.2 %collective-permute-start.4 = (f32[1,512]{1,0:T(1,128)S(1)}, f32[1,512]{1,0:T(1,128)S(1)}, u32[]{:S(2)}, u32[]{:S(2)}) collective-permute-start(f32[1,512]{1,0:T(1,128)S(1)} %get-tuple-element.131), channel_id=1, source_target_pairs={{8,0},{16,8},{24,16},{32,24},{40,32},{48,40},{56,48},{64,56},{72,6... | collective-permute-start | bytes 6152 | tf_op jit(solution)/shard_map/ppermute | solution.py:20
  27.5 12.0 %collective-permute-start.5 = (f32[1,512]{1,0:T(1,128)S(1)}, f32[1,512]{1,0:T(1,128)S(1)}, u32[]{:S(2)}, u32[]{:S(2)}) collective-permute-start(f32[1,512]{1,0:T(1,128)S(1)} %get-tuple-element.132), channel_id=1, source_target_pairs={{0,8},{8,16},{16,24},{24,32},{32,40},{40,48},{48,56},{56,64},{64,7... | collective-permute-start | bytes 6152 | tf_op jit(solution)/shard_map/ppermute | solution.py:19
  32.2 7.3 %collective-permute-start.6 = (f32[256,1]{1,0:T(8,128)S(1)}, f32[256,1]{1,0:T(8,128)S(1)}, u32[]{:S(2)}, u32[]{:S(2)}) collective-permute-start(f32[256,1]{1,0:T(8,128)S(1)} %get-tuple-element.130), channel_id=1, source_target_pairs={{1,0},{2,1},{3,2},{4,3},{5,4},{6,5},{7,6},{9,8},{10,9},{11,10},{12... | collective-permute-start | bytes 3080 | tf_op jit(solution)/shard_map/ppermute | solution.py:20
  33.5 6.0 %collective-permute-start.7 = (f32[256,1]{1,0:T(8,128)S(1)}, f32[256,1]{1,0:T(8,128)S(1)}, u32[]{:S(2)}, u32[]{:S(2)}) collective-permute-start(f32[256,1]{1,0:T(8,128)S(1)} %get-tuple-element.129), channel_id=1, source_target_pairs={{0,1},{1,2},{2,3},{3,4},{4,5},{5,6},{6,7},{8,9},{9,10},{10,11},{11... | collective-permute-start | bytes 3080 | tf_op jit(solution)/shard_map/ppermute | solution.py:19
  39.4 24.0 %copy-start.8 = (s32[128]{0:T(128)S(1)}, s32[128]{0:T(128)}, u32[]{:S(2)}) copy-start(s32[128]{0:T(128)} %param.11) | copy-start | bytes 1540
  40.2 0.8 copy-start.3
  41.7 21.7 %collective-permute-start.10 = (f32[256,1]{1,0:T(8,128)}, f32[256,1]{1,0:T(8,128)S(1)}, u32[]{:S(2)}, u32[]{:S(2)}) collective-permute-start(f32[256,1]{1,0:T(8,128)} %get-tuple-element.126), channel_id=1, source_target_pairs={{1,0},{2,1},{3,2},{4,3},{5,4},{6,5},{7,6},{9,8},{10,9},{11,10},{12... | collective-permute-start | bytes 3080 | tf_op jit(solution)/shard_map/ppermute | solution.py:20
  43.0 20.4 %collective-permute-start.11 = (f32[256,1]{1,0:T(8,128)S(1)}, f32[256,1]{1,0:T(8,128)S(1)}, u32[]{:S(2)}, u32[]{:S(2)}) collective-permute-start(f32[256,1]{1,0:T(8,128)S(1)} %get-tuple-element.125), channel_id=1, source_target_pairs={{0,1},{1,2},{2,3},{3,4},{4,5},{5,6},{6,7},{8,9},{9,10},{10,11},{11... | collective-permute-start | bytes 3080 | tf_op jit(solution)/shard_map/ppermute | solution.py:19
  47.1 1.0 copy-start.5
  48.0 116.9 %all-to-all-start = ((s32[1024,16,32]{0,2,1:T(8,128)}), s32[1024,16,32]{0,2,1:T(8,128)S(1)}, u32[]{:S(2)}, u32[]{:S(2)}) async-start(s32[1024,16,32]{0,2,1:T(8,128)} %bitcast), calls=%async_computation | async-start | bytes 4194304 | tf_op jit(solution)/shard_map/all_to_all | solution.py:88
  57.6 11.6 %collective-permute-start.8 = (f32[1,512]{1,0:T(1,128)S(1)}, f32[1,512]{1,0:T(1,128)S(1)}, u32[]{:S(2)}, u32[]{:S(2)}) collective-permute-start(f32[1,512]{1,0:T(1,128)S(1)} %get-tuple-element.127), channel_id=1, source_target_pairs={{8,0},{16,8},{24,16},{32,24},{40,32},{48,40},{56,48},{64,56},{72,6... | collective-permute-start | bytes 6152 | tf_op jit(solution)/shard_map/ppermute | solution.py:20
  58.8 10.4 %collective-permute-start.9 = (f32[1,512]{1,0:T(1,128)S(1)}, f32[1,512]{1,0:T(1,128)S(1)}, u32[]{:S(2)}, u32[]{:S(2)}) collective-permute-start(f32[1,512]{1,0:T(1,128)S(1)} %get-tuple-element.128), channel_id=1, source_target_pairs={{0,8},{8,16},{16,24},{24,32},{32,40},{40,48},{48,56},{56,64},{64,7... | collective-permute-start | bytes 6152 | tf_op jit(solution)/shard_map/ppermute | solution.py:19
  71.9 13.3 %copy-start.4 = (f32[256,512]{1,0:T(8,128)}, f32[256,512]{1,0:T(8,128)S(1)}, u32[]{:S(2)}) copy-start(f32[256,512]{1,0:T(8,128)S(1)} %fusion.44) | copy-start | bytes 1572868
  72.8 32.5 %collective-permute-start.14 = (f32[256,1]{1,0:T(8,128)}, f32[256,1]{1,0:T(8,128)S(1)}, u32[]{:S(2)}, u32[]{:S(2)}) collective-permute-start(f32[256,1]{1,0:T(8,128)} %get-tuple-element.122), channel_id=1, source_target_pairs={{1,0},{2,1},{3,2},{4,3},{5,4},{6,5},{7,6},{9,8},{10,9},{11,10},{12... | collective-permute-start | bytes 3080 | tf_op jit(solution)/shard_map/ppermute | solution.py:20
  74.1 31.2 %collective-permute-start.15 = (f32[256,1]{1,0:T(8,128)}, f32[256,1]{1,0:T(8,128)}, u32[]{:S(2)}, u32[]{:S(2)}) collective-permute-start(f32[256,1]{1,0:T(8,128)} %get-tuple-element.121), channel_id=1, source_target_pairs={{0,1},{1,2},{2,3},{3,4},{4,5},{5,6},{6,7},{8,9},{9,10},{10,11},{11... | collective-permute-start | bytes 3080 | tf_op jit(solution)/shard_map/ppermute | solution.py:19
  85.8 19.5 %collective-permute-start.12 = (f32[1,512]{1,0:T(1,128)}, f32[1,512]{1,0:T(1,128)S(1)}, u32[]{:S(2)}, u32[]{:S(2)}) collective-permute-start(f32[1,512]{1,0:T(1,128)} %get-tuple-element.123), channel_id=1, source_target_pairs={{8,0},{16,8},{24,16},{32,24},{40,32},{48,40},{56,48},{64,56},{72,6... | collective-permute-start | bytes 6152 | tf_op jit(solution)/shard_map/ppermute | solution.py:20
  87.0 18.2 %collective-permute-start.13 = (f32[1,512]{1,0:T(1,128)S(1)}, f32[1,512]{1,0:T(1,128)S(1)}, u32[]{:S(2)}, u32[]{:S(2)}) collective-permute-start(f32[1,512]{1,0:T(1,128)S(1)} %get-tuple-element.124), channel_id=1, source_target_pairs={{0,8},{8,16},{16,24},{24,32},{32,40},{40,48},{48,56},{56,64},{64,7... | collective-permute-start | bytes 6152 | tf_op jit(solution)/shard_map/ppermute | solution.py:19
  108.1 0.8 copy-start.6
where the time goes:
time: 313 us; the launch traced here: 311 us
  matrix products  78.2 us (25%)
  starting transfers between devices  68.7 us (22%)
  blocking collectives  62.4 us (20%)
  other arithmetic  51.4 us (16%)
  local copies, waits for them, and re-layouts  41.6 us (13%)
  waiting for transfers between devices  5.8 us (2%)
    dot_general x16, matrix products, one_block(): jnp.einsum('tpoh,pol->othl', left, right, preferred_element_type=jnp.floa...  78.2 us
    all_gather x1, blocking collectives, on_device(): every = lax.all_gather(sample, ('box', 'panel'), axis=1, tiled=True)  48.7 us
    ppermute x8, starting transfers between devices, padded(): lax.ppermute(last, axis, up)  39.4 us
    unnamed x25, local copies, waits for them, and re-layouts  14.5 us
    mul x16, other arithmetic, one_block(): amp_rows.astype(jnp.float32)[None, :, :] * sample[:, :, None]  14.3 us
    all_to_all x1, blocking collectives, on_device(): lax.all_to_all(finished, 'box', split_axis=1, concat_axis=0, tiled=True)  13.7 us
    dot_general x16, other arithmetic, one_block(): jnp.einsum('tpoh,pol->othl', left, right, preferred_element_type=jnp.floa...  13.6 us
    ppermute x8, starting transfers between devices, padded(): lax.ppermute(initial, axis, [(b, a) for a, b in up])  10.3 us
  transfers between devices with their start and end apart: 18, of which 1 were waited for; matrix products, arithmetic and copies ran while one was open for 12% of the time, Pallas kernels for 0%

commit v1 on v0

--- a/solution.py
+++ b/solution.py
@@ -83,7 +83,12 @@
         field = advance(extended, maskf, base_visc)
         taken.append(field.reshape(-1)[panel_cell])
     sample = jnp.stack(taken)
-    every = lax.all_gather(sample, ("box", "panel"), axis=1, tiled=True)
+    every = jnp.concatenate(
+        lax.all_to_all(
+            jnp.stack([sample] * lax.axis_size(("box", "panel"))), ("box", "panel"), 0, 0
+        ),
+        axis=1,
+    )
     amp_all = lax.all_to_all(amplitude, "box", split_axis=1, concat_axis=0, tiled=True)
     bin_all = lax.all_to_all(delay_bin, "box", split_axis=1, concat_axis=0, tiled=True)
     finished = signal_terms(amp_all, bin_all, every)

time: 313 us -> 300 us (0.958)
  blocking collectives: 62.4 us -> 12 us
  waiting for transfers between devices: 5.8 us -> 50.6 us
  local copies, waits for them, and re-layouts: 41.6 us -> 29.6 us
  starting transfers between devices: 68.7 us -> 74.1 us
    all_gather x1 -> x0, blocking collectives: 48.7 us -> none  [on_device(): every = lax.all_gather(sample, ('box', 'panel'), axis=1, tiled=True)]
    all_to_all x1, waiting for transfers between devices: 0.01 us -> 22.9 us  [on_device(): lax.all_to_all(delay_bin, 'box', split_axis=1, concat_axis=0, tiled=True)]
    all_to_all x0 -> x1, starting transfers between devices: none -> 18.6 us  [on_device(): lax.all_to_all(jnp.stack([sample] * lax.axis_size(('box', 'panel'))), ('b...]
    all_to_all x1, waiting for transfers between devices: 0.01 us -> 16.1 us  [on_device(): lax.all_to_all(amplitude, 'box', split_axis=1, concat_axis=0, tiled=True)]
    all_to_all x0 -> x1, waiting for transfers between devices: none -> 8.43 us  [on_device(): lax.all_to_all(jnp.stack([sample] * lax.axis_size(('box', 'panel'))), ('b...]
    unnamed x25 -> x22, local copies, waits for them, and re-layouts: 14.5 us -> 7.15 us
    all_to_all x1, starting transfers between devices: 10.3 us -> 3.65 us  [on_device(): lax.all_to_all(amplitude, 'box', split_axis=1, concat_axis=0, tiled=True)]
    ppermute x8, waiting for transfers between devices: 5.77 us -> 0.02 us  [padded(): lax.ppermute(initial, axis, [(b, a) for a, b in up])]
  transfers between devices with their start and end apart: 18 -> 19, of which waited for: 1 -> 6; matrix products, arithmetic and copies ran while one was open for 12% -> 5% of each run, Pallas kernels for 0% -> 0%
where the time goes in v1:
time: 300 us; the launch traced here: 298 us
  matrix products  78.3 us (26%)
  starting transfers between devices  74.1 us (25%)
  waiting for transfers between devices  50.6 us (17%)
  other arithmetic  50.3 us (17%)
  local copies, waits for them, and re-layouts  29.6 us (10%)
  blocking collectives  12 us (4%)
    dot_general x16, matrix products, one_block(): jnp.einsum('tpoh,pol->othl', left, right, preferred_element_type=jnp.floa...  78.3 us
    ppermute x8, starting transfers between devices, padded(): lax.ppermute(last, axis, up)  37.6 us
    all_to_all x1, waiting for transfers between devices, on_device(): lax.all_to_all(delay_bin, 'box', split_axis=1, concat_axis=0, tiled=True)  22.9 us
    all_to_all x1, starting transfers between devices, on_device(): lax.all_to_all(jnp.stack([sample] * lax.axis_size(('box', 'panel'))), ('b...  18.6 us
    all_to_all x1, waiting for transfers between devices, on_device(): lax.all_to_all(amplitude, 'box', split_axis=1, concat_axis=0, tiled=True)  16.1 us
    mul x16, other arithmetic, one_block(): amp_rows.astype(jnp.float32)[None, :, :] * sample[:, :, None]  14.3 us
    dot_general x16, other arithmetic, one_block(): jnp.einsum('tpoh,pol->othl', left, right, preferred_element_type=jnp.floa...  13.6 us
    all_to_all x1, blocking collectives, on_device(): lax.all_to_all(finished, 'box', split_axis=1, concat_axis=0, tiled=True)  12 us
  transfers between devices with their start and end apart: 19, of which 6 were waited for; matrix products, arithmetic and copies ran while one was open for 5% of the time, Pallas kernels for 0%

profile of v1, /device:TPU:0, one launch (start us, length us, event | category | flops | bytes accessed | tf_op | source)
XLA Modules:
  0.0 298.0 jit_solution(9250340820826021262)
XLA Ops:
  1.5 1.3 collective-permute-start
  2.8 4.6 %collective-permute-start.1 = (f32[1,512]{1,0:T(1,128)S(1)}, f32[1,512]{1,0:T(1,128)S(1)}, u32[]{:S(2)}, u32[]{:S(2)}) collective-permute-start(f32[1,512]{1,0:T(1,128)S(1)} %get-tuple-element.141), channel_id=1, source_target_pairs={{0,8},{8,16},{16,24},{24,32},{32,40},{40,48},{48,56},{56,64},{64,7... | collective-permute-start | bytes 6152 | tf_op jit(solution)/shard_map/ppermute | solution.py:19
  8.4 1.3 collective-permute-start.2
  9.7 3.0 %collective-permute-start.3 = (f32[256,1]{1,0:T(8,128)S(1)}, f32[256,1]{1,0:T(8,128)S(1)}, u32[]{:S(2)}, u32[]{:S(2)}) collective-permute-start(f32[256,1]{1,0:T(8,128)S(1)} %get-tuple-element.138), channel_id=1, source_target_pairs={{0,1},{1,2},{2,3},{3,4},{4,5},{5,6},{6,7},{8,9},{9,10},{10,11},{11... | collective-permute-start | bytes 3080 | tf_op jit(solution)/shard_map/ppermute | solution.py:19
  13.7 3.1 %fusion.80 = f32[256,512]{1,0:T(8,128)S(1)} fusion(f32[256,512]{1,0:T(8,128)} %param.8, f32[1,512]{1,0:T(1,128)S(1)} %collective-permute-done.1, f32[1,512]{1,0:T(1,128)S(1)} %collective-permute-done, f32[256,512]{1,0:T(8,128)} %param.10, f32[256,1]{1,0:T(8,128)S(1)} %collective-permute-done.2, f32[256,1]{1,0:T(8,128)S(1)} %collective-permute-done.3, ...), kind=kLoop, calls=%fused_computation.131 | loop fusion | flops 5242880 | bytes 2103296 | tf_op jit(solution)/shard_map/mul | solution.py:43
  16.9 1.3 collective-permute-start.4
  18.2 4.6 %collective-permute-start.5 = (f32[1,512]{1,0:T(1,128)S(1)}, f32[1,512]{1,0:T(1,128)S(1)}, u32[]{:S(2)}, u32[]{:S(2)}) collective-permute-start(f32[1,512]{1,0:T(1,128)S(1)} %get-tuple-element.137), channel_id=1, source_target_pairs={{0,8},{8,16},{16,24},{24,32},{32,40},{40,48},{48,56},{56,64},{64,7... | collective-permute-start | bytes 6152 | tf_op jit(solution)/shard_map/ppermute | solution.py:19
  22.8 1.3 collective-permute-start.6
  24.1 4.3 %collective-permute-start.7 = (f32[256,1]{1,0:T(8,128)S(1)}, f32[256,1]{1,0:T(8,128)S(1)}, u32[]{:S(2)}, u32[]{:S(2)}) collective-permute-start(f32[256,1]{1,0:T(8,128)S(1)} %get-tuple-element.134), channel_id=1, source_target_pairs={{0,1},{1,2},{2,3},{3,4},{4,5},{5,6},{6,7},{8,9},{9,10},{10,11},{11... | collective-permute-start | bytes 3080 | tf_op jit(solution)/shard_map/ppermute | solution.py:19
  29.4 2.0 fusion.62
  31.5 1.3 collective-permute-start.10
  32.8 6.3 %collective-permute-start.11 = (f32[256,1]{1,0:T(8,128)S(1)}, f32[256,1]{1,0:T(8,128)S(1)}, u32[]{:S(2)}, u32[]{:S(2)}) collective-permute-start(f32[256,1]{1,0:T(8,128)S(1)} %get-tuple-element.130), channel_id=1, source_target_pairs={{0,1},{1,2},{2,3},{3,4},{4,5},{5,6},{6,7},{8,9},{9,10},{10,11},{11... | collective-permute-start | bytes 3080 | tf_op jit(solution)/shard_map/ppermute | solution.py:19
  39.2 1.3 collective-permute-start.8
  40.5 4.5 %collective-permute-start.9 = (f32[1,512]{1,0:T(1,128)S(1)}, f32[1,512]{1,0:T(1,128)S(1)}, u32[]{:S(2)}, u32[]{:S(2)}) collective-permute-start(f32[1,512]{1,0:T(1,128)S(1)} %get-tuple-element.133), channel_id=1, source_target_pairs={{0,8},{8,16},{16,24},{24,32},{32,40},{40,48},{48,56},{56,64},{64,7... | collective-permute-start | bytes 6152 | tf_op jit(solution)/shard_map/ppermute | solution.py:19
  47.2 1.3 collective-permute-start.14
  48.5 4.0 %collective-permute-start.15 = (f32[256,1]{1,0:T(8,128)S(1)}, f32[256,1]{1,0:T(8,128)S(1)}, u32[]{:S(2)}, u32[]{:S(2)}) collective-permute-start(f32[256,1]{1,0:T(8,128)S(1)} %get-tuple-element.126), channel_id=1, source_target_pairs={{0,1},{1,2},{2,3},{3,4},{4,5},{5,6},{6,7},{8,9},{9,10},{10,11},{11... | collective-permute-start | bytes 3080 | tf_op jit(solution)/shard_map/ppermute | solution.py:19
  52.6 1.3 collective-permute-start.12
  53.9 6.2 %collective-permute-start.13 = (f32[1,512]{1,0:T(1,128)S(1)}, f32[1,512]{1,0:T(1,128)S(1)}, u32[]{:S(2)}, u32[]{:S(2)}) collective-permute-start(f32[1,512]{1,0:T(1,128)S(1)} %get-tuple-element.129), channel_id=1, source_target_pairs={{0,8},{8,16},{16,24},{24,32},{32,40},{40,48},{48,56},{56,64},{64,7... | collective-permute-start | bytes 6152 | tf_op jit(solution)/shard_map/ppermute | solution.py:19
  67.6 18.6 %all-to-all-start.2 = ((f32[128,4,128]{2,1,0:T(4,128)}), f32[128,4,128]{2,1,0:T(4,128)S(1)}, u32[]{:S(2)}, u32[]{:S(2)}) async-start(f32[128,4,128]{2,1,0:T(4,128)} %stack.17), calls=%async_computation.2 | async-start | bytes 524288 | tf_op jit(solution)/shard_map/all_to_all | solution.py:87
  86.3 2.3 copy.37
  88.5 8.4 %all-to-all-done.2 = f32[128,4,128]{2,1,0:T(4,128)S(1)} async-done(((f32[128,4,128]{2,1,0:T(4,128)}), f32[128,4,128]{2,1,0:T(4,128)S(1)}, u32[]{:S(2)}, u32[]{:S(2)}) %all-to-all-start.2) | async-done | bytes 262176 | tf_op jit(solution)/shard_map/all_to_all | solution.py:87
  97.0 3.7 %all-to-all-start.1 = ((bf16[1024,16,32]{0,2,1:T(8,128)(2,1)}), bf16[1024,16,32]{0,2,1:T(8,128)(2,1)S(1)}, u32[]{:S(2)}, u32[]{:S(2)}) async-start(bf16[1024,16,32]{0,2,1:T(8,128)(2,1)} %bitcast.3), calls=%async_computation.1 | async-start | bytes 2097152 | tf_op jit(solution)/shard_map/all_to_all | solution.py:92
  100.6 1.9 copy.35
  102.5 16.1 %all-to-all-done.1 = bf16[1024,16,32]{0,2,1:T(8,128)(2,1)S(1)} async-done(((bf16[1024,16,32]{0,2,1:T(8,128)(2,1)}), bf16[1024,16,32]{0,2,1:T(8,128)(2,1)S(1)}, u32[]{:S(2)}, u32[]{:S(2)}) %all-to-all-start.1) | async-done | bytes 1048608 | tf_op jit(solution)/shard_map/all_to_all | solution.py:92
  118.6 3.9 %all-to-all-start = ((s32[1024,16,32]{0,2,1:T(8,128)}), s32[1024,16,32]{0,2,1:T(8,128)S(1)}, u32[]{:S(2)}, u32[]{:S(2)}) async-start(s32[1024,16,32]{0,2,1:T(8,128)} %bitcast), calls=%async_computation | async-start | bytes 4194304 | tf_op jit(solution)/shard_map/all_to_all | solution.py:93
  123.5 1.6 copy.38
  125.0 2.6 reshape.103
  127.7 22.9 %all-to-all-done = s32[1024,16,32]{0,2,1:T(8,128)S(1)} async-done(((s32[1024,16,32]{0,2,1:T(8,128)}), s32[1024,16,32]{0,2,1:T(8,128)S(1)}, u32[]{:S(2)}, u32[]{:S(2)}) %all-to-all-start) | async-done | bytes 2097184 | tf_op jit(solution)/shard_map/all_to_all | solution.py:93
  150.6 2.6 copy.36
  153.2 3.1 %reshape.102 = s32[16384,16,2]{0,2,1:T(2,128)S(1)} reshape(s32[16,1024,32]{1,0,2:T(8,128)} %copy.36) | data formatting | bytes 4194304 | tf_op jit(solution)/shard_map/reshape | solution.py:52
  156.3 128.7 %while.13 = (s32[]{:T(128)}, f32[16,2,2048]{2,1,0:T(2,128)S(1)}, s32[16,16384,2]{1,2,0:T(2,128)S(1)}, bf16[16,16384,2]{1,2,0:T(2,128)(2,1)}, f32[4,128,128]{2,1,0:T(8,128)S(1)}, /*index=5*/s32[]{:T(128)}) while((s32[]{:T(128)}, f32[16,2,2048]{2,1,0:T(2,128)S(1)}, s32[16,16384,2]{1,2,0:T(2,128)S(1)}, ...), condition=%wide.region_1.2_spmd.clone, body=%wide.region_0.1_spmd.clone.sunk | while | flops 544616448 | bytes 12238737 | solution.py:73
  159.1 4.9 %fusion.114 = f32[2,4,16,128]{3,2,1,0:T(8,128)S(1)} fusion(s32[16384,2]{0,1:T(2,128)S(1)} %get-tuple-element.175, bf16[4,16384,2,16]{1,3,0,2:T(8,128)(2,1)S(1)} %fusion.113), kind=kOutput, calls=%fused_computation.8.clone.3 | convolution fusion | flops 541065216 | bytes 4390912 | tf_op jit(solution)/shard_map/while/body/eval_jaxpr/tpoh,pol->othl/dot_general | solution.py:66
  167.1 4.9 %fusion.114 = f32[2,4,16,128]{3,2,1,0:T(8,128)S(1)} fusion(s32[16384,2]{0,1:T(2,128)S(1)} %get-tuple-element.175, bf16[4,16384,2,16]{1,3,0,2:T(8,128)(2,1)S(1)} %fusion.113), kind=kOutput, calls=%fused_computation.8.clone.3 | convolution fusion | flops 541065216 | bytes 4390912 | tf_op jit(solution)/shard_map/while/body/eval_jaxpr/tpoh,pol->othl/dot_general | solution.py:66
  175.2 4.9 %fusion.114 = f32[2,4,16,128]{3,2,1,0:T(8,128)S(1)} fusion(s32[16384,2]{0,1:T(2,128)S(1)} %get-tuple-element.175, bf16[4,16384,2,16]{1,3,0,2:T(8,128)(2,1)S(1)} %fusion.113), kind=kOutput, calls=%fused_computation.8.clone.3 | convolution fusion | flops 541065216 | bytes 4390912 | tf_op jit(solution)/shard_map/while/body/eval_jaxpr/tpoh,pol->othl/dot_general | solution.py:66
  183.2 4.9 %fusion.114 = f32[2,4,16,128]{3,2,1,0:T(8,128)S(1)} fusion(s32[16384,2]{0,1:T(2,128)S(1)} %get-tuple-element.175, bf16[4,16384,2,16]{1,3,0,2:T(8,128)(2,1)S(1)} %fusion.113), kind=kOutput, calls=%fused_computation.8.clone.3 | convolution fusion | flops 541065216 | bytes 4390912 | tf_op jit(solution)/shard_map/while/body/eval_jaxpr/tpoh,pol->othl/dot_general | solution.py:66
  191.2 4.9 %fusion.114 = f32[2,4,16,128]{3,2,1,0:T(8,128)S(1)} fusion(s32[16384,2]{0,1:T(2,128)S(1)} %get-tuple-element.175, bf16[4,16384,2,16]{1,3,0,2:T(8,128)(2,1)S(1)} %fusion.113), kind=kOutput, calls=%fused_computation.8.clone.3 | convolution fusion | flops 541065216 | bytes 4390912 | tf_op jit(solution)/shard_map/while/body/eval_jaxpr/tpoh,pol->othl/dot_general | solution.py:66
  199.3 4.9 %fusion.114 = f32[2,4,16,128]{3,2,1,0:T(8,128)S(1)} fusion(s32[16384,2]{0,1:T(2,128)S(1)} %get-tuple-element.175, bf16[4,16384,2,16]{1,3,0,2:T(8,128)(2,1)S(1)} %fusion.113), kind=kOutput, calls=%fused_computation.8.clone.3 | convolution fusion | flops 541065216 | bytes 4390912 | tf_op jit(solution)/shard_map/while/body/eval_jaxpr/tpoh,pol->othl/dot_general | solution.py:66
  207.3 4.9 %fusion.114 = f32[2,4,16,128]{3,2,1,0:T(8,128)S(1)} fusion(s32[16384,2]{0,1:T(2,128)S(1)} %get-tuple-element.175, bf16[4,16384,2,16]{1,3,0,2:T(8,128)(2,1)S(1)} %fusion.113), kind=kOutput, calls=%fused_computation.8.clone.3 | convolution fusion | flops 541065216 | bytes 4390912 | tf_op jit(solution)/shard_map/while/body/eval_jaxpr/tpoh,pol->othl/dot_general | solution.py:66
  215.4 4.9 %fusion.114 = f32[2,4,16,128]{3,2,1,0:T(8,128)S(1)} fusion(s32[16384,2]{0,1:T(2,128)S(1)} %get-tuple-element.175, bf16[4,16384,2,16]{1,3,0,2:T(8,128)(2,1)S(1)} %fusion.113), kind=kOutput, calls=%fused_computation.8.clone.3 | convolution fusion | flops 541065216 | bytes 4390912 | tf_op jit(solution)/shard_map/while/body/eval_jaxpr/tpoh,pol->othl/dot_general | solution.py:66
  223.4 4.9 %fusion.114 = f32[2,4,16,128]{3,2,1,0:T(8,128)S(1)} fusion(s32[16384,2]{0,1:T(2,128)S(1)} %get-tuple-element.175, bf16[4,16384,2,16]{1,3,0,2:T(8,128)(2,1)S(1)} %fusion.113), kind=kOutput, calls=%fused_computation.8.clone.3 | convolution fusion | flops 541065216 | bytes 4390912 | tf_op jit(solution)/shard_map/while/body/eval_jaxpr/tpoh,pol->othl/dot_general | solution.py:66
  231.5 4.9 %fusion.114 = f32[2,4,16,128]{3,2,1,0:T(8,128)S(1)} fusion(s32[16384,2]{0,1:T(2,128)S(1)} %get-tuple-element.175, bf16[4,16384,2,16]{1,3,0,2:T(8,128)(2,1)S(1)} %fusion.113), kind=kOutput, calls=%fused_computation.8.clone.3 | convolution fusion | flops 541065216 | bytes 4390912 | tf_op jit(solution)/shard_map/while/body/eval_jaxpr/tpoh,pol->othl/dot_general | solution.py:66
  239.5 4.9 %fusion.114 = f32[2,4,16,128]{3,2,1,0:T(8,128)S(1)} fusion(s32[16384,2]{0,1:T(2,128)S(1)} %get-tuple-element.175, bf16[4,16384,2,16]{1,3,0,2:T(8,128)(2,1)S(1)} %fusion.113), kind=kOutput, calls=%fused_computation.8.clone.3 | convolution fusion | flops 541065216 | bytes 4390912 | tf_op jit(solution)/shard_map/while/body/eval_jaxpr/tpoh,pol->othl/dot_general | solution.py:66
  247.5 4.9 %fusion.114 = f32[2,4,16,128]{3,2,1,0:T(8,128)S(1)} fusion(s32[16384,2]{0,1:T(2,128)S(1)} %get-tuple-element.175, bf16[4,16384,2,16]{1,3,0,2:T(8,128)(2,1)S(1)} %fusion.113), kind=kOutput, calls=%fused_computation.8.clone.3 | convolution fusion | flops 541065216 | bytes 4390912 | tf_op jit(solution)/shard_map/while/body/eval_jaxpr/tpoh,pol->othl/dot_general | solution.py:66
  255.6 4.9 %fusion.114 = f32[2,4,16,128]{3,2,1,0:T(8,128)S(1)} fusion(s32[16384,2]{0,1:T(2,128)S(1)} %get-tuple-element.175, bf16[4,16384,2,16]{1,3,0,2:T(8,128)(2,1)S(1)} %fusion.113), kind=kOutput, calls=%fused_computation.8.clone.3 | convolution fusion | flops 541065216 | bytes 4390912 | tf_op jit(solution)/shard_map/while/body/eval_jaxpr/tpoh,pol->othl/dot_general | solution.py:66
  263.6 4.9 %fusion.114 = f32[2,4,16,128]{3,2,1,0:T(8,128)S(1)} fusion(s32[16384,2]{0,1:T(2,128)S(1)} %get-tuple-element.175, bf16[4,16384,2,16]{1,3,0,2:T(8,128)(2,1)S(1)} %fusion.113), kind=kOutput, calls=%fused_computation.8.clone.3 | convolution fusion | flops 541065216 | bytes 4390912 | tf_op jit(solution)/shard_map/while/body/eval_jaxpr/tpoh,pol->othl/dot_general | solution.py:66
  271.7 4.9 %fusion.114 = f32[2,4,16,128]{3,2,1,0:T(8,128)S(1)} fusion(s32[16384,2]{0,1:T(2,128)S(1)} %get-tuple-element.175, bf16[4,16384,2,16]{1,3,0,2:T(8,128)(2,1)S(1)} %fusion.113), kind=kOutput, calls=%fused_computation.8.clone.3 | convolution fusion | flops 541065216 | bytes 4390912 | tf_op jit(solution)/shard_map/while/body/eval_jaxpr/tpoh,pol->othl/dot_general | solution.py:66
  279.7 4.9 %fusion.114 = f32[2,4,16,128]{3,2,1,0:T(8,128)S(1)} fusion(s32[16384,2]{0,1:T(2,128)S(1)} %get-tuple-element.175, bf16[4,16384,2,16]{1,3,0,2:T(8,128)(2,1)S(1)} %fusion.113), kind=kOutput, calls=%fused_computation.8.clone.3 | convolution fusion | flops 541065216 | bytes 4390912 | tf_op jit(solution)/shard_map/while/body/eval_jaxpr/tpoh,pol->othl/dot_general | solution.py:66
  285.2 12.0 %all_to_all.56 = f32[32,16,128]{2,0,1:T(8,128)S(1)} all-to-all(f32[32,16,128]{2,0,1:T(8,128)S(1)} %copy.40), channel_id=1, replica_groups=mesh['box'=16,'panel'=8] {'box'}, dimensions={1} | all-to-all | bytes 524288 | tf_op jit(solution)/shard_map/all_to_all | solution.py:95
  (297 shorter events, 64.0 us)
Async XLA Ops:
  0.6 45.7 %copy-start = (f32[256,512]{1,0:T(8,128)S(1)}, f32[256,512]{1,0:T(8,128)}, u32[]{:S(2)}) copy-start(f32[256,512]{1,0:T(8,128)} %param.10) | copy-start | bytes 1572868
  0.6 45.7 %copy-start.1 = (s32[256,512]{1,0:T(8,128)S(1)}, s32[256,512]{1,0:T(8,128)}, u32[]{:S(2)}) copy-start(s32[256,512]{1,0:T(8,128)} %param.9) | copy-start | bytes 1572868
  0.7 44.4 %copy-start.6 = (s32[128]{0:T(128)S(1)}, s32[128]{0:T(128)}, u32[]{:S(2)}) copy-start(s32[128]{0:T(128)} %param.11) | copy-start | bytes 1540
  1.5 12.2 %collective-permute-start = (f32[1,512]{1,0:T(1,128)S(1)}, f32[1,512]{1,0:T(1,128)S(1)}, u32[]{:S(2)}, u32[]{:S(2)}) collective-permute-start(f32[1,512]{1,0:T(1,128)S(1)} %get-tuple-element.140), channel_id=1, source_target_pairs={{8,0},{16,8},{24,16},{32,24},{40,32},{48,40},{56,48},{64,56},{72,6... | collective-permute-start | bytes 6152 | tf_op jit(solution)/shard_map/ppermute | solution.py:20
  2.8 11.0 %collective-permute-start.1 = (f32[1,512]{1,0:T(1,128)S(1)}, f32[1,512]{1,0:T(1,128)S(1)}, u32[]{:S(2)}, u32[]{:S(2)}) collective-permute-start(f32[1,512]{1,0:T(1,128)S(1)} %get-tuple-element.141), channel_id=1, source_target_pairs={{0,8},{8,16},{16,24},{24,32},{32,40},{40,48},{48,56},{56,64},{64,7... | collective-permute-start | bytes 6152 | tf_op jit(solution)/shard_map/ppermute | solution.py:19
  8.4 4.3 %collective-permute-start.2 = (f32[256,1]{1,0:T(8,128)S(1)}, f32[256,1]{1,0:T(8,128)S(1)}, u32[]{:S(2)}, u32[]{:S(2)}) collective-permute-start(f32[256,1]{1,0:T(8,128)S(1)} %get-tuple-element.139), channel_id=1, source_target_pairs={{1,0},{2,1},{3,2},{4,3},{5,4},{6,5},{7,6},{9,8},{10,9},{11,10},{12... | collective-permute-start | bytes 3080 | tf_op jit(solution)/shard_map/ppermute | solution.py:20
  9.7 4.0 %collective-permute-start.3 = (f32[256,1]{1,0:T(8,128)S(1)}, f32[256,1]{1,0:T(8,128)S(1)}, u32[]{:S(2)}, u32[]{:S(2)}) collective-permute-start(f32[256,1]{1,0:T(8,128)S(1)} %get-tuple-element.138), channel_id=1, source_target_pairs={{0,1},{1,2},{2,3},{3,4},{4,5},{5,6},{6,7},{8,9},{9,10},{10,11},{11... | collective-permute-start | bytes 3080 | tf_op jit(solution)/shard_map/ppermute | solution.py:19
  16.9 12.6 %collective-permute-start.4 = (f32[1,512]{1,0:T(1,128)S(1)}, f32[1,512]{1,0:T(1,128)S(1)}, u32[]{:S(2)}, u32[]{:S(2)}) collective-permute-start(f32[1,512]{1,0:T(1,128)S(1)} %get-tuple-element.136), channel_id=1, source_target_pairs={{8,0},{16,8},{24,16},{32,24},{40,32},{48,40},{56,48},{64,56},{72,6... | collective-permute-start | bytes 6152 | tf_op jit(solution)/shard_map/ppermute | solution.py:20
  18.2 11.3 %collective-permute-start.5 = (f32[1,512]{1,0:T(1,128)S(1)}, f32[1,512]{1,0:T(1,128)S(1)}, u32[]{:S(2)}, u32[]{:S(2)}) collective-permute-start(f32[1,512]{1,0:T(1,128)S(1)} %get-tuple-element.137), channel_id=1, source_target_pairs={{0,8},{8,16},{16,24},{24,32},{32,40},{40,48},{48,56},{56,64},{64,7... | collective-permute-start | bytes 6152 | tf_op jit(solution)/shard_map/ppermute | solution.py:19
  22.8 5.6 %collective-permute-start.6 = (f32[256,1]{1,0:T(8,128)S(1)}, f32[256,1]{1,0:T(8,128)S(1)}, u32[]{:S(2)}, u32[]{:S(2)}) collective-permute-start(f32[256,1]{1,0:T(8,128)S(1)} %get-tuple-element.135), channel_id=1, source_target_pairs={{1,0},{2,1},{3,2},{4,3},{5,4},{6,5},{7,6},{9,8},{10,9},{11,10},{12... | collective-permute-start | bytes 3080 | tf_op jit(solution)/shard_map/ppermute | solution.py:20
  24.1 5.3 %collective-permute-start.7 = (f32[256,1]{1,0:T(8,128)S(1)}, f32[256,1]{1,0:T(8,128)S(1)}, u32[]{:S(2)}, u32[]{:S(2)}) collective-permute-start(f32[256,1]{1,0:T(8,128)S(1)} %get-tuple-element.134), channel_id=1, source_target_pairs={{0,1},{1,2},{2,3},{3,4},{4,5},{5,6},{6,7},{8,9},{9,10},{10,11},{11... | collective-permute-start | bytes 3080 | tf_op jit(solution)/shard_map/ppermute | solution.py:19
  31.5 13.5 %collective-permute-start.10 = (f32[256,1]{1,0:T(8,128)S(1)}, f32[256,1]{1,0:T(8,128)S(1)}, u32[]{:S(2)}, u32[]{:S(2)}) collective-permute-start(f32[256,1]{1,0:T(8,128)S(1)} %get-tuple-element.131), channel_id=1, source_target_pairs={{1,0},{2,1},{3,2},{4,3},{5,4},{6,5},{7,6},{9,8},{10,9},{11,10},{12... | collective-permute-start | bytes 3080 | tf_op jit(solution)/shard_map/ppermute | solution.py:20
  32.8 12.2 %collective-permute-start.11 = (f32[256,1]{1,0:T(8,128)S(1)}, f32[256,1]{1,0:T(8,128)S(1)}, u32[]{:S(2)}, u32[]{:S(2)}) collective-permute-start(f32[256,1]{1,0:T(8,128)S(1)} %get-tuple-element.130), channel_id=1, source_target_pairs={{0,1},{1,2},{2,3},{3,4},{4,5},{5,6},{6,7},{8,9},{9,10},{10,11},{11... | collective-permute-start | bytes 3080 | tf_op jit(solution)/shard_map/ppermute | solution.py:19
  39.2 5.9 %collective-permute-start.8 = (f32[1,512]{1,0:T(1,128)S(1)}, f32[1,512]{1,0:T(1,128)S(1)}, u32[]{:S(2)}, u32[]{:S(2)}) collective-permute-start(f32[1,512]{1,0:T(1,128)S(1)} %get-tuple-element.132), channel_id=1, source_target_pairs={{8,0},{16,8},{24,16},{32,24},{40,32},{48,40},{56,48},{64,56},{72,6... | collective-permute-start | bytes 6152 | tf_op jit(solution)/shard_map/ppermute | solution.py:20
  40.5 5.8 %collective-permute-start.9 = (f32[1,512]{1,0:T(1,128)S(1)}, f32[1,512]{1,0:T(1,128)S(1)}, u32[]{:S(2)}, u32[]{:S(2)}) collective-permute-start(f32[1,512]{1,0:T(1,128)S(1)} %get-tuple-element.133), channel_id=1, source_target_pairs={{0,8},{8,16},{16,24},{24,32},{32,40},{40,48},{48,56},{56,64},{64,7... | collective-permute-start | bytes 6152 | tf_op jit(solution)/shard_map/ppermute | solution.py:19
  47.2 16.7 %collective-permute-start.14 = (f32[256,1]{1,0:T(8,128)S(1)}, f32[256,1]{1,0:T(8,128)S(1)}, u32[]{:S(2)}, u32[]{:S(2)}) collective-permute-start(f32[256,1]{1,0:T(8,128)S(1)} %get-tuple-element.127), channel_id=1, source_target_pairs={{1,0},{2,1},{3,2},{4,3},{5,4},{6,5},{7,6},{9,8},{10,9},{11,10},{12... | collective-permute-start | bytes 3080 | tf_op jit(solution)/shard_map/ppermute | solution.py:20
  48.5 15.5 %collective-permute-start.15 = (f32[256,1]{1,0:T(8,128)S(1)}, f32[256,1]{1,0:T(8,128)S(1)}, u32[]{:S(2)}, u32[]{:S(2)}) collective-permute-start(f32[256,1]{1,0:T(8,128)S(1)} %get-tuple-element.126), channel_id=1, source_target_pairs={{0,1},{1,2},{2,3},{3,4},{4,5},{5,6},{6,7},{8,9},{9,10},{10,11},{11... | collective-permute-start | bytes 3080 | tf_op jit(solution)/shard_map/ppermute | solution.py:19
  52.6 11.4 %collective-permute-start.12 = (f32[1,512]{1,0:T(1,128)S(1)}, f32[1,512]{1,0:T(1,128)S(1)}, u32[]{:S(2)}, u32[]{:S(2)}) collective-permute-start(f32[1,512]{1,0:T(1,128)S(1)} %get-tuple-element.128), channel_id=1, source_target_pairs={{8,0},{16,8},{24,16},{32,24},{40,32},{48,40},{56,48},{64,56},{72,6... | collective-permute-start | bytes 6152 | tf_op jit(solution)/shard_map/ppermute | solution.py:20
  53.9 10.1 %collective-permute-start.13 = (f32[1,512]{1,0:T(1,128)S(1)}, f32[1,512]{1,0:T(1,128)S(1)}, u32[]{:S(2)}, u32[]{:S(2)}) collective-permute-start(f32[1,512]{1,0:T(1,128)S(1)} %get-tuple-element.129), channel_id=1, source_target_pairs={{0,8},{8,16},{16,24},{24,32},{32,40},{40,48},{48,56},{56,64},{64,7... | collective-permute-start | bytes 6152 | tf_op jit(solution)/shard_map/ppermute | solution.py:19
  64.8 0.8 copy-start.3
  64.8 35.8 %copy-start.2 = (s32[1024,512]{1,0:T(8,128)S(1)}, s32[1024,512]{1,0:T(8,128)}, u32[]{:S(2)}) copy-start(s32[1024,512]{1,0:T(8,128)} %param.13) | copy-start | bytes 6291460
  67.6 29.3 %all-to-all-start.2 = ((f32[128,4,128]{2,1,0:T(4,128)}), f32[128,4,128]{2,1,0:T(4,128)S(1)}, u32[]{:S(2)}, u32[]{:S(2)}) async-start(f32[128,4,128]{2,1,0:T(4,128)} %stack.17), calls=%async_computation.2 | async-start | bytes 524288 | tf_op jit(solution)/shard_map/all_to_all | solution.py:87
  97.0 25.5 %copy-start.4 = (f32[128,4,128]{2,1,0:T(4,128)}, f32[128,4,128]{2,1,0:T(4,128)S(1)}, u32[]{:S(2)}) copy-start(f32[128,4,128]{2,1,0:T(4,128)S(1)} %all-to-all-done.2) | copy-start | bytes 786436
  97.0 21.6 %all-to-all-start.1 = ((bf16[1024,16,32]{0,2,1:T(8,128)(2,1)}), bf16[1024,16,32]{0,2,1:T(8,128)(2,1)S(1)}, u32[]{:S(2)}, u32[]{:S(2)}) async-start(bf16[1024,16,32]{0,2,1:T(8,128)(2,1)} %bitcast.3), calls=%async_computation.1 | async-start | bytes 2097152 | tf_op jit(solution)/shard_map/all_to_all | solution.py:92
  118.6 32.0 %all-to-all-start = ((s32[1024,16,32]{0,2,1:T(8,128)}), s32[1024,16,32]{0,2,1:T(8,128)S(1)}, u32[]{:S(2)}, u32[]{:S(2)}) async-start(s32[1024,16,32]{0,2,1:T(8,128)} %bitcast), calls=%async_computation | async-start | bytes 4194304 | tf_op jit(solution)/shard_map/all_to_all | solution.py:93
  153.2 3.1 %copy-start.5 = (f32[16,2,2048]{2,1,0:T(2,128)S(1)}, f32[16,2,2048]{2,1,0:T(2,128)}, u32[]{:S(2)}) copy-start(f32[16,2,2048]{2,1,0:T(2,128)} %custom-call.8) | copy-start | bytes 786436
